TPU v7x, 32 devices: a whole 2x2x4 slice. The times are simulated.
32 devices in a mesh: obs: 8 (over z, x), chan: 4 (over y, core).
Axes of the slice: x: 2, y: 2, z: 4, core: 2. Of those that a mesh axis runs over, the one named last changes fastest.
Arguments:
- departures: bfloat16 [8192, 16384], P('chan', 'obs'), may hold values from -8 to 8
- predictors: bfloat16 [10, 16384], P(None, 'obs'), may hold values from -3 to 3
- inv_band: bfloat16 [63, 8192], P(None, 'chan'), may hold values from -1 to 2.5
- band_id: int32 [8192], replicated, may hold values from 0 to 340, never falling along the last dimension, each value on 1 to 32 neighbouring positions
- line_counts: int32 [128], P('obs'), may hold values from 24 to 128
Outputs:
- gram: float32 [100, 8192], P(None, ('chan', 'obs'))
- rhs: float32 [10, 8192], P(None, ('chan', 'obs'))
Inputs may be any that keep to these rules, and one draw needn't show every extreme that they name: `band_id`: band numbers never fall along the channels; a band spans 1 to 32 channels. `line_counts`: slots of a scan line at or beyond its count are empty.
All inputs are finite; a program needn't handle non-finite values.
Results may differ from a plain program's by a relative error of at most 0.00062.
Values may be sent and summed in bfloat16 or wider, within the bound.
A program may use at most 64 MiB of HBM per device.

v0:
```python
import functools

import jax
import jax.numpy as jnp
import numpy as np
from jax import lax
from jax.experimental import pallas as pl
from jax.experimental.pallas import tpu as pltpu
from jax.sharding import PartitionSpec as P

huber_edge = 1.0
LANES = 128
HALO = 32
TILE = 128
OBS_CHUNK = 2048
MESH = pl.DeviceIdType.MESH


def mirror_rows(count):
    rows = []
    for first in range(count):
        for second in range(count):
            low = min(first, second)
            high = max(first, second)
            rows.append(low * count - low * (low - 1) // 2 + high - low)
    return rows


def peer(axis, index):
    if axis == "obs":
        return (index, lax.axis_index("chan"))
    return (lax.axis_index("obs"), index)


def kernel(n_obs, n_chan, scatter, dep, pred, inv, ids, counts, *rest):
    if scatter:
        gram_out, rhs_out = rest[:2]
        rest = rest[2:]
    else:
        part_out = rest[0]
        rest = rest[1:]
    (
        window,
        pred_in,
        inv_in,
        ids_in,
        counts_in,
        wide,
        table,
        flip,
        bands,
        stage,
        landed_x,
        landed_z,
        total,
        small_sem,
        load_sem,
        halo_send,
        halo_recv,
        x_send,
        x_recv,
        z_send,
        z_recv,
    ) = rest
    own, obs_dev = dep.shape
    preds = pred.shape[0]
    offsets = inv.shape[0]
    half = offsets // 2
    upper = preds * (preds + 1) // 2
    blocks, rows, width = stage.shape
    tiles = width // TILE
    pairs = blocks // 2
    lines = counts.shape[0]
    slots = obs_dev // lines
    me = lax.axis_index("obs")
    chan = lax.axis_index("chan")
    right = lax.rem(chan + 1, n_chan)
    left = lax.rem(chan + n_chan - 1, n_chan)
    spot = lax.rem(me, blocks)
    col = lax.rem(spot, 2)
    lev = lax.div(spot, 2)
    stride = jnp.where(lev < pairs // 2, 1, pairs - 1)

    def level_at(turn):
        return lax.rem(lev + stride * (turn + 1), pairs)

    def for_partner(step):
        odd = lax.rem(step, 2) == 1
        return jnp.logical_or(step == 0, jnp.logical_and(odd, step < blocks - 1))

    def turn_at(step):
        return jnp.where(for_partner(step), lax.div(step + 1, 2), lax.div(jnp.maximum(step - 1, 0), 2))

    def block_at(step):
        side = jnp.where(for_partner(step), 1 - col, col)
        return 2 * level_at(turn_at(step)) + side

    barrier = pltpu.get_barrier_semaphore()
    for index in (left, right):
        pl.semaphore_signal(barrier, inc=1, device_id=peer("chan", index), device_id_type=MESH)
    greeted = 2
    if scatter:
        partner = me + 1 - 2 * col
        pl.semaphore_signal(barrier, inc=1, device_id=peer("obs", partner), device_id_type=MESH)
        for turn in range(pairs - 1):
            index = 2 * level_at(turn) + col
            pl.semaphore_signal(barrier, inc=1, device_id=peer("obs", index), device_id_type=MESH)
        greeted += pairs

    base = pl.multiple_of(chan * own, own)
    smalls = [
        pltpu.make_async_copy(pred, pred_in, small_sem.at[0]),
        pltpu.make_async_copy(counts, counts_in, small_sem.at[1]),
        pltpu.make_async_copy(inv, inv_in, small_sem.at[2]),
        pltpu.make_async_copy(
            ids.at[:, pl.ds(base, own)], ids_in.at[:, pl.ds(LANES, own)], small_sem.at[3]
        ),
    ]
    before = pltpu.make_async_copy(
        ids.at[:, pl.ds(pl.multiple_of(jnp.maximum(base - LANES, 0), LANES), LANES)],
        ids_in.at[:, pl.ds(0, LANES)],
        small_sem.at[4],
    )
    after = pltpu.make_async_copy(
        ids.at[:, pl.ds(pl.multiple_of(jnp.minimum(base + own, own * n_chan - LANES), LANES), LANES)],
        ids_in.at[:, pl.ds(LANES + own, LANES)],
        small_sem.at[5],
    )
    for copy in smalls:
        copy.start()
    before.start()
    after.start()

    origin = block_at(0) + blocks - jnp.where(stride == 1, 1, blocks - 1)
    hop = jnp.where(stride == 1, 1, blocks - 1)

    def load(place):
        chunk = lax.rem(origin + hop * place, blocks)
        start = pl.multiple_of(chunk * width, width)
        return pltpu.make_async_copy(
            dep.at[pl.ds(start, width), :],
            window.at[pl.ds(start + HALO, width), :],
            load_sem.at[place],
        )

    def start_load(place, carry):
        load(place).start()
        return carry

    lax.fori_loop(0, blocks, start_load, 0)

    smalls[0].wait()
    smalls[1].wait()
    values = pred_in[...].astype(jnp.float32)
    wide[upper + preds :, :] = jnp.zeros((LANES - upper - preds, obs_dev), jnp.float32)
    first_row = 0
    for first in range(preds):
        count = preds - first
        wide[first_row : first_row + count, :] = values[first:, :] * values[first : first + 1, :]
        first_row += count
    wide[upper : upper + preds, :] = values
    lane = lax.broadcasted_iota(jnp.int32, (slots, LANES), 1)

    def turn_line(line, carry):
        at = pl.ds(pl.multiple_of(line * slots, slots), slots)
        slot = lax.broadcasted_iota(jnp.int32, (LANES, slots), 1)
        live = jnp.where(slot < counts_in[line], wide[:, at], 0.0)
        turned = live.T
        per = OBS_CHUNK // slots
        spot_q = pl.multiple_of(lax.div(line, per) * 2 * OBS_CHUNK + lax.rem(line, per) * slots, slots)
        table[pl.ds(spot_q, slots), :] = jnp.where(lane < upper, turned, 0.0).astype(jnp.bfloat16)
        table[pl.ds(spot_q + OBS_CHUNK, slots), :] = jnp.where(lane >= upper, turned, 0.0).astype(
            jnp.bfloat16
        )
        return carry

    lax.fori_loop(0, lines, turn_line, 0, unroll=4)

    pl.semaphore_wait(barrier, greeted)
    to_left = pltpu.make_async_remote_copy(
        src_ref=dep.at[pl.ds(0, HALO), :],
        dst_ref=window.at[pl.ds(own + HALO, HALO), :],
        send_sem=halo_send.at[0],
        recv_sem=halo_recv.at[0],
        device_id=peer("chan", left),
        device_id_type=MESH,
    )
    to_right = pltpu.make_async_remote_copy(
        src_ref=dep.at[pl.ds(own - HALO, HALO), :],
        dst_ref=window.at[pl.ds(0, HALO), :],
        send_sem=halo_send.at[1],
        recv_sem=halo_recv.at[1],
        device_id=peer("chan", right),
        device_id_type=MESH,
    )
    to_left.start()
    to_right.start()

    smalls[2].wait()
    smalls[3].wait()
    before.wait()
    after.wait()

    @pl.when(chan == 0)
    def _():
        ids_in[:, 0:LANES] = jnp.full((1, LANES), -1, jnp.int32)

    @pl.when(chan == n_chan - 1)
    def _():
        ids_in[:, LANES + own :] = jnp.full((1, LANES), -1, jnp.int32)

    flip[...] = jnp.zeros_like(flip)

    def build(block):
        for part in range(tiles):
            first = pl.multiple_of(block * width + part * TILE, TILE)
            near = ids_in[:, pl.ds(first, 3 * TILE)].astype(jnp.float32)
            flip[part, 0:offsets, :] = inv_in[:, pl.ds(first, TILE)].astype(jnp.float32)
            flip[part, 64:65, :] = near[:, TILE : 2 * TILE]
            turned = flip[part].T
            own_id = turned[:, 64:65]
            place = lax.broadcasted_iota(jnp.int32, turned.shape, 1)
            turned = jnp.where(place < offsets, turned, 0.0)
            skewed = pltpu.roll(
                jnp.concatenate([turned, jnp.zeros_like(turned)], axis=1),
                HALO - half,
                1,
                stride=1,
                stride_axis=0,
            )
            same = near[:, TILE - HALO : 3 * TILE - HALO] == own_id
            bands[part * TILE : (part + 1) * TILE, :] = jnp.where(same, skewed, 0.0).astype(
                jnp.bfloat16
            )

    def send_x(turn):
        return pltpu.make_async_remote_copy(
            src_ref=stage.at[turn],
            dst_ref=landed_x.at[turn],
            send_sem=x_send.at[turn],
            recv_sem=x_recv.at[turn],
            device_id=peer("obs", partner),
            device_id_type=MESH,
        )

    def send_z(turn):
        return pltpu.make_async_remote_copy(
            src_ref=stage.at[pairs + turn],
            dst_ref=landed_z.at[lev],
            send_sem=z_send.at[turn],
            recv_sem=z_recv.at[lev],
            device_id=peer("obs", 2 * level_at(turn) + col),
            device_id_type=MESH,
        )

    def from_z(turn):
        sender = level_at(turn)
        return pltpu.make_async_remote_copy(
            src_ref=stage.at[pairs],
            dst_ref=landed_z.at[sender],
            send_sem=z_send.at[0],
            recv_sem=z_recv.at[sender],
            device_id=peer("obs", 2 * sender + col),
            device_id_type=MESH,
        )

    for place in range(3):
        load(place).wait()
    build(block_at(0))

    def one_block(step, carry):
        block = block_at(step)

        @pl.when(step == 1)
        def _():
            for place in range(3, 5):
                load(place).wait()

        @pl.when(step == 2)
        def _():
            for place in range(5, blocks):
                load(place).wait()

        @pl.when(block == blocks - 1)
        def _():
            to_left.wait_recv()

        @pl.when(block == 0)
        def _():
            to_right.wait_recv()

        start = pl.multiple_of(block * width, width)
        extent = TILE + 2 * HALO
        sums = jnp.zeros((width, LANES), jnp.float32)
        matrices = [bands[part * TILE : (part + 1) * TILE, 0:extent] for part in range(tiles)]
        for at in range(0, obs_dev, OBS_CHUNK):
            parts = []
            for part in range(tiles):
                first = pl.multiple_of(start + part * TILE, TILE)
                weighted = jnp.dot(
                    matrices[part],
                    window[pl.ds(first, extent), at : at + OBS_CHUNK],
                    preferred_element_type=jnp.float32,
                )
                ratio = huber_edge / jnp.maximum(jnp.abs(weighted), huber_edge)
                qc_weight = ratio.astype(jnp.bfloat16)
                scaled = jnp.clip(weighted, -huber_edge, huber_edge).astype(jnp.bfloat16)
                parts.append(jnp.concatenate([qc_weight, scaled], axis=1))
            sums += jnp.dot(
                jnp.concatenate(parts, axis=0),
                table[2 * at : 2 * (at + OBS_CHUNK), :],
                preferred_element_type=jnp.float32,
            )
        build(block_at(jnp.minimum(step + 1, blocks - 1)))
        result = sums.T[:rows, :]
        if not scatter:
            part_out[:, pl.ds(start, width)] = result
            return carry
        turn = turn_at(step)

        @pl.when(for_partner(step))
        def _():
            stage[turn] = result
            send_x(turn).start()

        @pl.when(jnp.logical_not(for_partner(step)))
        def _():
            send_x(turn).wait_recv()
            stage[pairs + turn] = result + landed_x[turn]

            @pl.when(step < blocks - 1)
            def _():
                send_z(turn).start()

        return carry

    lax.fori_loop(0, blocks, one_block, 0)
    to_left.wait_send()
    to_right.wait_send()

    if scatter:
        sums = stage[blocks - 1]
        for turn in range(pairs - 2, -1, -1):
            from_z(turn).wait_recv()
            sums = sums + landed_z[level_at(turn)]
        total[...] = sums * (1.0 / float(obs_dev * n_obs))
        for row, source in enumerate(mirror_rows(preds)):
            gram_out[row : row + 1, :] = total[source : source + 1, :]
        rhs_out[...] = total[upper : upper + preds, :]
        for turn in range(pairs):
            send_x(turn).wait_send()
        for turn in range(pairs - 1):
            send_z(turn).wait_send()


def on_device(departures, predictors, inv_band, band_id, line_counts):
    own, obs_dev = departures.shape
    preds = predictors.shape[0]
    upper = preds * (preds + 1) // 2
    n_obs = lax.axis_size("obs")
    n_chan = lax.axis_size("chan")
    share = own // n_obs
    scatter = share % TILE == 0 and n_obs % 2 == 0
    blocks = n_obs if scatter else own // (2 * TILE)
    width = own // blocks
    rows = -(-(upper + preds) // 8) * 8
    if scatter:
        out_shape = (
            pltpu.VMEM((preds * preds, share), jnp.float32),
            pltpu.VMEM((preds, share), jnp.float32),
        )
    else:
        out_shape = (jax.ShapeDtypeStruct((rows, own), jnp.float32),)
    vmem = pl.BlockSpec(memory_space=pltpu.VMEM)
    hbm = pl.BlockSpec(memory_space=pltpu.HBM)
    pairs = blocks // 2
    landing = (pairs, rows, width) if scatter else (1, 8, LANES)
    dma = pltpu.SemaphoreType.DMA
    outs = pl.pallas_call(
        functools.partial(kernel, n_obs, n_chan, scatter),
        out_shape=out_shape,
        in_specs=[hbm] * 5,
        out_specs=tuple(vmem for _ in out_shape),
        scratch_shapes=[
            pltpu.VMEM((own + 2 * HALO, obs_dev), jnp.bfloat16),
            pltpu.VMEM(predictors.shape, jnp.bfloat16),
            pltpu.VMEM(inv_band.shape, jnp.bfloat16),
            pltpu.VMEM((1, own + 2 * LANES), jnp.int32),
            pltpu.SMEM(line_counts.shape, jnp.int32),
            pltpu.VMEM((LANES, obs_dev), jnp.float32),
            pltpu.VMEM((2 * obs_dev, LANES), jnp.bfloat16),
            pltpu.VMEM((width // TILE, LANES, TILE), jnp.float32),
            pltpu.VMEM((width, 2 * TILE), jnp.bfloat16),
            pltpu.VMEM((blocks, rows, width), jnp.float32),
            pltpu.VMEM(landing, jnp.float32),
            pltpu.VMEM(landing, jnp.float32),
            pltpu.VMEM((rows, width), jnp.float32),
            dma((6,)),
            dma((blocks,)),
            dma((2,)),
            dma((2,)),
            dma((pairs,)),
            dma((pairs,)),
            dma((pairs,)),
            dma((pairs,)),
        ],
        compiler_params=pltpu.CompilerParams(
            collective_id=0,
            has_side_effects=True,
            vmem_limit_bytes=67043328 - 120 * 1024,
        ),
        name="normal_equations",
    )(departures, predictors, inv_band, band_id[None, :], line_counts)
    if scatter:
        return outs[0], outs[1]
    factor = 1.0 / float(obs_dev * n_obs)
    part = lax.psum_scatter(outs[0], "obs", scatter_dimension=1, tiled=True) * factor
    mirror = np.array(mirror_rows(preds))
    return part[mirror], part[upper : upper + preds]


def solution(mesh):
    in_specs = (P("chan", "obs"), P(None, "obs"), P(None, "chan"), P(), P("obs"))
    out_specs = (P(None, ("chan", "obs")), P(None, ("chan", "obs")))
    return jax.shard_map(
        on_device, mesh=mesh, in_specs=in_specs, out_specs=out_specs, check_vma=False
    )
```

profile of v0, /device:TPU:0, one launch (start us, length us, event | category | flops | bytes accessed | tf_op | source)
XLA Modules:
  0.0 23.5 jit_solution(2700838260960938131)
XLA Ops:
  0.6 21.6 %normal_equations.1 = (f32[100,256]{1,0:T(8,128)S(1)}, f32[10,256]{1,0:T(8,128)S(1)}) custom-call(bf16[2048,2048]{1,0:T(8,128)(2,1)} %dep.1, bf16[10,2048]{1,0:T(8,128)(2,1)} %pred_.1, bf16[63,2048]{1,0:T(8,128)(2,1)} %inv.1, s32[1,8192]{1,0:T(1,128)} %bitcast.1, s32[16]{0:T(128)} %counts.1), custom_call_target="tpu_custom_call" | custom-call | tf_op jit(solution)/shard_map/normal_equations/pallas_call | solution.py:379
  22.2 0.6 %copy.9 = f32[100,256]{1,0:T(8,128)} copy(f32[100,256]{1,0:T(8,128)S(1)} %get-tuple-element.2) | data formatting | bytes 204800
  22.9 0.6 %copy.10 = f32[10,256]{1,0:T(8,128)} copy(f32[10,256]{1,0:T(8,128)S(1)} %get-tuple-element.3) | data formatting | bytes 20480
where the time goes:
time: 23.6 us; the launch traced here: 23.5 us
  Pallas kernels  21.6 us (92%)
  local copies, waits for them, and re-layouts  1.25 us (5%)
  between operations  0.64 us (3%)
    pallas_call x1, Pallas kernels, on_device(): pl.pallas_call(functools.partial(kernel, n_obs, n_chan, scatter), out_sha...  21.6 us
    unnamed x2, local copies, waits for them, and re-layouts  1.25 us

commit v1 on v0

v1 whole, which is shorter than its diff:
```python
import functools

import jax
import jax.numpy as jnp
import numpy as np
from jax import lax
from jax.experimental import pallas as pl
from jax.experimental.pallas import tpu as pltpu
from jax.sharding import PartitionSpec as P

huber_edge = 1.0
LANES = 128
HALO = 32
TILE = 128
WIDTH = 2 * TILE
OBS_TILE = 256
CODE = 32512.0
MESH = pl.DeviceIdType.MESH


def mirror_rows(count):
    rows = []
    for first in range(count):
        for second in range(count):
            low = min(first, second)
            high = max(first, second)
            rows.append(low * count - low * (low - 1) // 2 + high - low)
    return rows


def padded(count, unit):
    return -(-count // unit) * unit


def peer(axis, index):
    if axis == "obs":
        return (index, lax.axis_index("chan"))
    return (lax.axis_index("obs"), index)


def kernel(n_obs, n_chan, scatter, dep, pred, inv, ids, counts, *rest):
    if scatter:
        gram_out, rhs_out = rest[:2]
        rest = rest[2:]
    else:
        part_out = rest[0]
        rest = rest[1:]
    (
        window,
        pred_in,
        inv_in,
        ids_in,
        counts_in,
        wide,
        pairs_t,
        preds_t,
        flip,
        bands,
        turned_w,
        mine,
        x_code,
        z_code,
        landed_x,
        landed_z,
        total,
        small_sem,
        load_sem,
        halo_send,
        halo_recv,
        x_send,
        x_recv,
        z_send,
        z_recv,
    ) = rest
    own, obs_dev = dep.shape
    preds = pred.shape[0]
    offsets = inv.shape[0]
    half = offsets // 2
    upper = preds * (preds + 1) // 2
    pad = padded(upper, 8)
    tall = pairs_t.shape[0]
    flat = preds_t.shape[0]
    blocks = own // WIDTH
    levels = blocks // 2
    stages = obs_dev // (2 * OBS_TILE)
    lines = counts.shape[0]
    slots = obs_dev // lines
    me = lax.axis_index("obs")
    chan = lax.axis_index("chan")
    right = lax.rem(chan + 1, n_chan)
    left = lax.rem(chan + n_chan - 1, n_chan)
    if scatter:
        col = lax.rem(me, 2)
        lev = lax.div(me, 2)
        partner = me + 1 - 2 * col
    else:
        col = 1
        lev = levels - 1
        partner = me
    early = lev == 0

    def level_at(turn):
        turn = jnp.int32(turn)
        return jnp.where(turn == levels - 1, lev, jnp.where(turn >= lev, turn + 1, turn))

    def first_col(turn):
        later = 1 - col if scatter else 0
        return jnp.where(turn == 0, jnp.where(early, col, 1), later)

    def block_at(step):
        step = jnp.int32(step)
        turn = lax.div(step, 2)
        first = first_col(turn)
        return 2 * level_at(turn) + jnp.where(lax.rem(step, 2) == 0, first, 1 - first)

    def for_partner(step):
        return lax.rem(block_at(step), 2) != col

    barrier = pltpu.get_barrier_semaphore()
    for index in (left, right):
        pl.semaphore_signal(barrier, inc=1, device_id=peer("chan", index), device_id_type=MESH)
    greeted = 2
    if scatter:
        pl.semaphore_signal(barrier, inc=1, device_id=peer("obs", partner), device_id_type=MESH)
        for turn in range(levels - 1):
            index = 2 * level_at(turn) + col
            pl.semaphore_signal(barrier, inc=1, device_id=peer("obs", index), device_id_type=MESH)
        greeted += levels

    base = pl.multiple_of(chan * own, own)
    smalls = [
        pltpu.make_async_copy(pred, pred_in, small_sem.at[0]),
        pltpu.make_async_copy(counts, counts_in, small_sem.at[1]),
        pltpu.make_async_copy(inv, inv_in, small_sem.at[2]),
        pltpu.make_async_copy(
            ids.at[:, pl.ds(base, own)], ids_in.at[:, pl.ds(LANES, own)], small_sem.at[3]
        ),
        pltpu.make_async_copy(
            ids.at[:, pl.ds(pl.multiple_of(jnp.maximum(base - LANES, 0), LANES), LANES)],
            ids_in.at[:, pl.ds(0, LANES)],
            small_sem.at[4],
        ),
        pltpu.make_async_copy(
            ids.at[
                :, pl.ds(pl.multiple_of(jnp.minimum(base + own, own * n_chan - LANES), LANES), LANES)
            ],
            ids_in.at[:, pl.ds(LANES + own, LANES)],
            small_sem.at[5],
        ),
    ]
    for copy in smalls:
        copy.start()

    def load(place):
        chunk = lax.rem(jnp.where(early, 1, 0) + place, blocks)
        start = pl.multiple_of(chunk * WIDTH, WIDTH)
        return pltpu.make_async_copy(
            dep.at[pl.ds(start, WIDTH), :],
            window.at[pl.ds(start + HALO, WIDTH), :],
            load_sem.at[place],
        )

    for place in range(blocks):
        load(place).start()

    to_left = pltpu.make_async_remote_copy(
        src_ref=dep.at[pl.ds(0, HALO), :],
        dst_ref=window.at[pl.ds(own + HALO, HALO), :],
        send_sem=halo_send.at[0],
        recv_sem=halo_recv.at[0],
        device_id=peer("chan", left),
        device_id_type=MESH,
    )
    to_right = pltpu.make_async_remote_copy(
        src_ref=dep.at[pl.ds(own - HALO, HALO), :],
        dst_ref=window.at[pl.ds(0, HALO), :],
        send_sem=halo_send.at[1],
        recv_sem=halo_recv.at[1],
        device_id=peer("chan", right),
        device_id_type=MESH,
    )

    def meet():
        pl.semaphore_wait(barrier, greeted)
        to_left.start()
        to_right.start()

    pl.when(jnp.logical_not(early))(meet)

    window[own + 2 * HALO :, :] = jnp.zeros((window.shape[0] - own - 2 * HALO, obs_dev), window.dtype)
    flip[...] = jnp.zeros_like(flip)
    wide[...] = jnp.zeros_like(wide)

    smalls[0].wait()
    smalls[1].wait()
    values = pred_in[...].astype(jnp.float32)
    first_row = 0
    for first in range(preds):
        count = preds - first
        wide[first_row : first_row + count, :] = values[first:, :] * values[first : first + 1, :]
        first_row += count
    wide[tall : tall + preds, :] = values

    def mask_line(line, carry):
        at = pl.ds(pl.multiple_of(line * slots, slots), slots)
        slot = lax.broadcasted_iota(jnp.int32, (tall + flat, slots), 1)
        live = jnp.where(slot < counts_in[line], wide[:, at], 0.0).astype(jnp.bfloat16)
        pairs_t[:, at] = live[:tall, :]
        preds_t[:, at] = live[tall:, :]
        return carry

    lax.fori_loop(0, lines, mask_line, 0, unroll=4)

    for copy in smalls[2:]:
        copy.wait()

    @pl.when(chan == 0)
    def _():
        ids_in[:, 0:LANES] = jnp.full((1, LANES), -1, jnp.int32)

    @pl.when(chan == n_chan - 1)
    def _():
        ids_in[:, LANES + own :] = jnp.full((1, LANES), -1, jnp.int32)

    def build(block, side):
        for part in range(2):
            first = pl.multiple_of(block * WIDTH + part * TILE, TILE)
            near = ids_in[:, pl.ds(first, 3 * TILE)].astype(jnp.float32)
            flip[part, 0:offsets, :] = inv_in[:, pl.ds(first, TILE)].astype(jnp.float32)
            flip[part, 64:65, :] = near[:, TILE : 2 * TILE]
            turned = flip[part].T
            own_id = turned[:, 64:65]
            place = lax.broadcasted_iota(jnp.int32, turned.shape, 1)
            turned = jnp.where(place < offsets, turned, 0.0)
            skewed = pltpu.roll(
                jnp.concatenate([turned, jnp.zeros_like(turned)], axis=1),
                HALO - half,
                1,
                stride=1,
                stride_axis=0,
            )
            same = near[:, TILE - HALO : 3 * TILE - HALO] == own_id
            bands[side, part * TILE : (part + 1) * TILE, :] = jnp.where(same, skewed, 0.0).astype(
                jnp.bfloat16
            )

    def send_x(turn):
        return pltpu.make_async_remote_copy(
            src_ref=x_code.at[turn],
            dst_ref=landed_x.at[turn],
            send_sem=x_send.at[turn],
            recv_sem=x_recv.at[turn],
            device_id=peer("obs", partner),
            device_id_type=MESH,
        )

    def send_z(turn):
        return pltpu.make_async_remote_copy(
            src_ref=z_code.at[turn],
            dst_ref=landed_z.at[lev],
            send_sem=z_send.at[turn],
            recv_sem=z_recv.at[lev],
            device_id=peer("obs", 2 * level_at(turn) + col),
            device_id_type=MESH,
        )

    def from_z(turn):
        sender = level_at(turn)
        return pltpu.make_async_remote_copy(
            src_ref=z_code.at[0],
            dst_ref=landed_z.at[sender],
            send_sem=z_send.at[0],
            recv_sem=z_recv.at[sender],
            device_id=peer("obs", 2 * sender + col),
            device_id_type=MESH,
        )

    def encode(sums):
        gram = sums[:pad]
        rhs = sums[pad:]

        def grade(part):
            most = jnp.max(jnp.abs(part), axis=0, keepdims=True)
            return jnp.ceil(jnp.log2(jnp.maximum(most, 1e-30)))

        gram_grade = grade(gram)
        rhs_grade = grade(rhs)
        row = lax.broadcasted_iota(jnp.int32, rhs.shape, 0)
        gram = gram * (jnp.exp2(-gram_grade) * CODE)
        rhs = rhs * (jnp.exp2(-rhs_grade) * CODE)
        rhs = jnp.where(row == preds, gram_grade, rhs)
        rhs = jnp.where(row == preds + 1, rhs_grade, rhs)
        return jnp.round(jnp.concatenate([gram, rhs], axis=0)).astype(jnp.int32).astype(jnp.int16)

    def decode(code):
        values = code.astype(jnp.int32).astype(jnp.float32)
        gram_scale = jnp.exp2(values[pad + preds : pad + preds + 1]) * (1.0 / CODE)
        rhs_scale = jnp.exp2(values[pad + preds + 1 : pad + preds + 2]) * (1.0 / CODE)
        return jnp.concatenate([values[:pad] * gram_scale, values[pad:] * rhs_scale], axis=0)

    def pass_on(turn):
        send_x(turn).wait_recv()
        z_code[turn] = encode(mine[turn] + decode(landed_x[turn]))
        send_z(turn).start()

    def accumulated(*accs):
        narrow = [[accs[4 * mxu + 2 * side : 4 * mxu + 2 * side + 2] for side in range(2)] for mxu in range(2)]
        tall_acc = [accs[8 + 2 * mxu : 10 + 2 * mxu] for mxu in range(2)]
        flat_acc = [accs[12 + 2 * mxu : 14 + 2 * mxu] for mxu in range(2)]

        def weigh(block, band, stage):
            start = pl.multiple_of(block * WIDTH, WIDTH)
            for mxu in range(2):
                at = (2 * stage + mxu) * OBS_TILE
                for part in range(2):
                    first = pl.multiple_of(start + part * TILE, TILE)
                    pltpu.matmul_push_rhs(
                        window[pl.ds(first, 2 * TILE), at : at + OBS_TILE],
                        staging_register=part,
                        mxu_index=mxu,
                    )
                    pltpu.matmul_acc_lhs(
                        narrow[mxu][stage % 2][part],
                        bands[band, part * TILE : (part + 1) * TILE, :],
                        load_staged_rhs=part,
                    )

        def turn_over(stage):
            for mxu in range(2):
                for part in range(2):
                    weighted = pltpu.matmul_pop(narrow[mxu][stage % 2][part])
                    turned_w[stage % 2, mxu, :, part * TILE : (part + 1) * TILE] = weighted.astype(
                        jnp.bfloat16
                    ).T

        def gather(side, stage):
            edge = jnp.bfloat16(huber_edge)
            for mxu in range(2):
                at = (2 * stage + mxu) * OBS_TILE
                weighted = turned_w[stage % 2, mxu]
                qc_weight = edge / jnp.maximum(jnp.abs(weighted), edge)
                scaled = jnp.clip(weighted, -edge, edge)
                pltpu.matmul_push_rhs(qc_weight, staging_register=0, mxu_index=mxu)
                pltpu.matmul_acc_lhs(
                    tall_acc[mxu][side], pairs_t[:, at : at + OBS_TILE], load_staged_rhs=0
                )
                pltpu.matmul_push_rhs(scaled, staging_register=1, mxu_index=mxu)
                pltpu.matmul_acc_lhs(
                    flat_acc[mxu][side], preds_t[:, at : at + OBS_TILE], load_staged_rhs=1
                )

        def result(side):
            gram = pltpu.matmul_pop(tall_acc[0][side]) + pltpu.matmul_pop(tall_acc[1][side])
            rhs = pltpu.matmul_pop(flat_acc[0][side]) + pltpu.matmul_pop(flat_acc[1][side])
            return jnp.concatenate([gram[:pad], rhs], axis=0)

        def deliver(step, sums):
            if not scatter:
                start = pl.multiple_of(block_at(step) * WIDTH, WIDTH)
                part_out[:, pl.ds(start, WIDTH)] = sums
                return
            turn = lax.div(step, 2)
            theirs = for_partner(step)

            @pl.when(theirs)
            def _():
                x_code[turn] = encode(sums)
                send_x(turn).start()

            @pl.when(jnp.logical_not(theirs))
            def _():
                mine[turn] = sums

        for acc in accs:
            pltpu.matmul_pop(acc)
        for place in range(4):
            load(place).wait()
        build(block_at(0), 0)
        weigh(block_at(0), 0, 0)
        weigh(block_at(0), 0, 1)
        turn_over(0)

        def one_turn(turn, carry):
            for side in range(2):
                step = 2 * turn + side
                block = block_at(step)
                following = block_at(jnp.minimum(step + 1, blocks - 1))
                more = step + 1 < blocks
                middle = stages // 2
                build(following, 1 - side)
                for stage in range(stages):
                    if stage == middle:
                        sums = result(1 - side)
                        if side == 1:

                            @pl.when(turn == 0)
                            def _():
                                for place in range(4, blocks):
                                    load(place).wait()

                            deliver(step - 1, sums)
                        else:

                            @pl.when(jnp.logical_and(early, turn == 1))
                            def _():
                                meet()

                            @pl.when(turn > 0)
                            def _():
                                deliver(step - 1, sums)

                            if scatter:

                                @pl.when(turn > 1)
                                def _():
                                    pass_on(turn - 2)

                        @pl.when(jnp.logical_and(more, following == 0))
                        def _():
                            to_right.wait_recv()

                        @pl.when(jnp.logical_and(more, following == blocks - 1))
                        def _():
                            to_left.wait_recv()

                    ahead = stage + 2
                    if ahead < stages:
                        weigh(block, side, ahead)
                    else:
                        weigh(following, 1 - side, ahead - stages)
                    turn_over((stage + 1) % stages)
                    gather(side, stage)
            return carry

        lax.fori_loop(0, levels, one_turn, 0)
        for mxu in range(2):
            for part in range(2):
                for side in range(2):
                    pltpu.matmul_pop(narrow[mxu][side][part])
        deliver(blocks - 1, result(1))

    pl.run_scoped(accumulated, *acc_list(tall, flat))
    to_left.wait_send()
    to_right.wait_send()

    if scatter:
        pass_on(levels - 2)
        last = levels - 1
        send_x(last).wait_recv()
        sums = mine[last] + decode(landed_x[last])
        for turn in range(levels - 1):
            from_z(turn).wait_recv()
            sums = sums + decode(landed_z[level_at(turn)])
        total[...] = sums * (1.0 / float(obs_dev * n_obs))
        for row, source in enumerate(mirror_rows(preds)):
            gram_out[row : row + 1, :] = total[source : source + 1, :]
        rhs_out[...] = total[pad : pad + preds, :]
        for turn in range(levels):
            send_x(turn).wait_send()
        for turn in range(levels - 1):
            send_z(turn).wait_send()


def acc_list(tall, flat):
    specs = []
    for rows, copies in ((TILE, 4), (tall, 2), (flat, 2)):
        for mxu in range(2):
            specs += [pltpu.ACC(mxu)((rows, OBS_TILE), jnp.float32)] * copies
    return specs


def on_device(departures, predictors, inv_band, band_id, line_counts):
    own, obs_dev = departures.shape
    preds = predictors.shape[0]
    upper = preds * (preds + 1) // 2
    n_obs = lax.axis_size("obs")
    n_chan = lax.axis_size("chan")
    share = own // n_obs
    blocks = own // WIDTH
    scatter = share == WIDTH and n_obs % 2 == 0 and n_obs >= 8
    pad = padded(upper, 8)
    tall = padded(upper, 16)
    flat = padded(preds + 2, 16)
    rows = pad + flat
    if scatter:
        out_shape = (
            pltpu.VMEM((preds * preds, share), jnp.float32),
            pltpu.VMEM((preds, share), jnp.float32),
        )
    else:
        out_shape = (jax.ShapeDtypeStruct((rows, own), jnp.float32),)
    vmem = pl.BlockSpec(memory_space=pltpu.VMEM)
    hbm = pl.BlockSpec(memory_space=pltpu.HBM)
    levels = blocks // 2
    kept = (levels, rows, WIDTH) if scatter else (1, 8, LANES)
    dma = pltpu.SemaphoreType.DMA
    outs = pl.pallas_call(
        functools.partial(kernel, n_obs, n_chan, scatter),
        out_shape=out_shape,
        in_specs=[hbm] * 5,
        out_specs=tuple(vmem for _ in out_shape),
        scratch_shapes=[
            pltpu.VMEM((own + 4 * HALO, obs_dev), jnp.bfloat16),
            pltpu.VMEM(predictors.shape, jnp.bfloat16),
            pltpu.VMEM(inv_band.shape, jnp.bfloat16),
            pltpu.VMEM((1, own + 2 * LANES), jnp.int32),
            pltpu.SMEM(line_counts.shape, jnp.int32),
            pltpu.VMEM((tall + flat, obs_dev), jnp.float32),
            pltpu.VMEM((tall, obs_dev), jnp.bfloat16),
            pltpu.VMEM((flat, obs_dev), jnp.bfloat16),
            pltpu.VMEM((2, LANES, TILE), jnp.float32),
            pltpu.VMEM((2, WIDTH, 2 * TILE), jnp.bfloat16),
            pltpu.VMEM((2, 2, OBS_TILE, WIDTH), jnp.bfloat16),
            pltpu.VMEM(kept, jnp.float32),
            pltpu.VMEM(kept, jnp.int16),
            pltpu.VMEM(kept, jnp.int16),
            pltpu.VMEM(kept, jnp.int16),
            pltpu.VMEM(kept, jnp.int16),
            pltpu.VMEM((rows, WIDTH), jnp.float32),
            dma((6,)),
            dma((blocks,)),
            dma((2,)),
            dma((2,)),
            dma((levels,)),
            dma((levels,)),
            dma((levels,)),
            dma((levels,)),
        ],
        compiler_params=pltpu.CompilerParams(
            collective_id=0,
            has_side_effects=True,
            vmem_limit_bytes=67043328 - 120 * 1024,
        ),
        name="normal_equations",
    )(departures, predictors, inv_band, band_id[None, :], line_counts)
    if scatter:
        return outs[0], outs[1]
    factor = 1.0 / float(obs_dev * n_obs)
    part = lax.psum_scatter(outs[0], "obs", scatter_dimension=1, tiled=True) * factor
    mirror = np.array(mirror_rows(preds))
    return part[mirror], part[pad : pad + preds]


def solution(mesh):
    in_specs = (P("chan", "obs"), P(None, "obs"), P(None, "chan"), P(), P("obs"))
    out_specs = (P(None, ("chan", "obs")), P(None, ("chan", "obs")))
    return jax.shard_map(
        on_device, mesh=mesh, in_specs=in_specs, out_specs=out_specs, check_vma=False
    )
```

time: 23.6 us -> 21.5 us (0.911)
  the two profiles are of different devices: /device:TPU:0 before, /device:TPU:20 now
where the time goes in v1:
time: 21.5 us; the launch traced here: 21.4 us
  Pallas kernels  19.5 us (91%)
  local copies, waits for them, and re-layouts  1.25 us (6%)
  between operations  0.64 us (3%)
    pallas_call x1, Pallas kernels, on_device(): pl.pallas_call(functools.partial(kernel, n_obs, n_chan, scatter), out_sha...  19.5 us
    unnamed x2, local copies, waits for them, and re-layouts  1.25 us

profile of v1, /device:TPU:20, one launch (start us, length us, event | category | flops | bytes accessed | tf_op | source)
XLA Modules:
  0.0 21.4 jit_solution(7100577547506206987)
XLA Ops:
  0.6 19.5 %normal_equations.1 = (f32[100,256]{1,0:T(8,128)S(1)}, f32[10,256]{1,0:T(8,128)S(1)}) custom-call(bf16[2048,2048]{1,0:T(8,128)(2,1)} %dep.1, bf16[10,2048]{1,0:T(8,128)(2,1)} %pred_.1, bf16[63,2048]{1,0:T(8,128)(2,1)} %inv.1, s32[1,8192]{1,0:T(1,128)} %bitcast.1, s32[16]{0:T(128)} %counts.1), custom_call_target="tpu_custom_call" | custom-call | tf_op jit(solution)/shard_map/normal_equations/pallas_call | solution.py:497
  20.1 0.6 %copy.9 = f32[100,256]{1,0:T(8,128)} copy(f32[100,256]{1,0:T(8,128)S(1)} %get-tuple-element.2) | data formatting | bytes 204800
  20.8 0.6 %copy.10 = f32[10,256]{1,0:T(8,128)} copy(f32[10,256]{1,0:T(8,128)S(1)} %get-tuple-element.3) | data formatting | bytes 20480

commit v2 on v1

--- a/solution.py
+++ b/solution.py
@@ -47,6 +47,7 @@
         rest = rest[1:]
     (
         window,
+        strip,
         pred_in,
         inv_in,
         ids_in,
@@ -57,7 +58,6 @@
         flip,
         bands,
         turned_w,
-        mine,
         x_code,
         z_code,
         landed_x,
@@ -97,24 +97,41 @@
         col = 1
         lev = levels - 1
         partner = me
-    early = lev == 0
+    early = lev == 0 if scatter else me < 0
 
     def level_at(turn):
         turn = jnp.int32(turn)
         return jnp.where(turn == levels - 1, lev, jnp.where(turn >= lev, turn + 1, turn))
 
-    def first_col(turn):
-        later = 1 - col if scatter else 0
-        return jnp.where(turn == 0, jnp.where(early, col, 1), later)
+    def level_of(step):
+        step = jnp.int32(step)
+        if not scatter:
+            return lax.div(step, 2)
+        late_first = jnp.where(step < 2, 1 - step, step)
+        late_last = jnp.where(step == levels - 1, 0, step + 1)
+        late_mid = jnp.where(
+            step == levels - 1, levels - 1, jnp.where(step == levels - 2, 0, step + 1)
+        )
+        lead = jnp.where(
+            early,
+            jnp.where(col == 0, late_mid, late_last),
+            jnp.where(col == 0, step, late_first),
+        )
+        return jnp.where(step < levels, lead, level_at(step - levels))
 
     def block_at(step):
         step = jnp.int32(step)
-        turn = lax.div(step, 2)
-        first = first_col(turn)
-        return 2 * level_at(turn) + jnp.where(lax.rem(step, 2) == 0, first, 1 - first)
-
-    def for_partner(step):
-        return lax.rem(block_at(step), 2) != col
+        if not scatter:
+            return jnp.where(step < 2, 1 - step, step)
+        return 2 * level_of(step) + jnp.where(step < levels, 1 - col, col)
+
+    def chunk_at(place):
+        if not scatter:
+            return place
+        turned_on = jnp.where(place < 3, place + 1, jnp.where(place == 3, 0, place))
+        return jnp.where(
+            early, lax.rem(2 - col + place, blocks), jnp.where(col == 0, place, turned_on)
+        )
 
     barrier = pltpu.get_barrier_semaphore()
     for index in (left, right):
@@ -152,7 +169,7 @@
         copy.start()
 
     def load(place):
-        chunk = lax.rem(jnp.where(early, 1, 0) + place, blocks)
+        chunk = chunk_at(jnp.int32(place))
         start = pl.multiple_of(chunk * WIDTH, WIDTH)
         return pltpu.make_async_copy(
             dep.at[pl.ds(start, WIDTH), :],
@@ -160,11 +177,17 @@
             load_sem.at[place],
         )
 
-    for place in range(blocks):
+    strips = [
+        pltpu.make_async_copy(dep.at[pl.ds(0, HALO), :], strip.at[0], small_sem.at[6]),
+        pltpu.make_async_copy(dep.at[pl.ds(own - HALO, HALO), :], strip.at[1], small_sem.at[7]),
+    ]
+    for copy in strips:
+        copy.start()
+    for place in range(3):
         load(place).start()
 
     to_left = pltpu.make_async_remote_copy(
-        src_ref=dep.at[pl.ds(0, HALO), :],
+        src_ref=strip.at[0],
         dst_ref=window.at[pl.ds(own + HALO, HALO), :],
         send_sem=halo_send.at[0],
         recv_sem=halo_recv.at[0],
@@ -172,7 +195,7 @@
         device_id_type=MESH,
     )
     to_right = pltpu.make_async_remote_copy(
-        src_ref=dep.at[pl.ds(own - HALO, HALO), :],
+        src_ref=strip.at[1],
         dst_ref=window.at[pl.ds(0, HALO), :],
         send_sem=halo_send.at[1],
         recv_sem=halo_recv.at[1],
@@ -182,17 +205,27 @@
 
     def meet():
         pl.semaphore_wait(barrier, greeted)
-        to_left.start()
-        to_right.start()
-
-    pl.when(jnp.logical_not(early))(meet)
-
+        pl.when(chan > 0)(to_left.start)
+        pl.when(chan < n_chan - 1)(to_right.start)
+
+    rim = jnp.zeros((HALO, obs_dev), window.dtype)
     window[own + 2 * HALO :, :] = jnp.zeros((window.shape[0] - own - 2 * HALO, obs_dev), window.dtype)
+
+    @pl.when(chan == 0)
+    def _():
+        window[:HALO, :] = rim
+
+    @pl.when(chan == n_chan - 1)
+    def _():
+        window[own + HALO : own + 2 * HALO, :] = rim
+
     flip[...] = jnp.zeros_like(flip)
     wide[...] = jnp.zeros_like(wide)
 
     smalls[0].wait()
     smalls[1].wait()
+    for place in range(3, blocks):
+        load(place).start()
     values = pred_in[...].astype(jnp.float32)
     first_row = 0
     for first in range(preds):
@@ -244,12 +277,12 @@
                 jnp.bfloat16
             )
 
-    def send_x(turn):
+    def send_x(step, level):
         return pltpu.make_async_remote_copy(
-            src_ref=x_code.at[turn],
-            dst_ref=landed_x.at[turn],
-            send_sem=x_send.at[turn],
-            recv_sem=x_recv.at[turn],
+            src_ref=x_code.at[step],
+            dst_ref=landed_x.at[level],
+            send_sem=x_send.at[step],
+            recv_sem=x_recv.at[level],
             device_id=peer("obs", partner),
             device_id_type=MESH,
         )
@@ -297,11 +330,6 @@
         gram_scale = jnp.exp2(values[pad + preds : pad + preds + 1]) * (1.0 / CODE)
         rhs_scale = jnp.exp2(values[pad + preds + 1 : pad + preds + 2]) * (1.0 / CODE)
         return jnp.concatenate([values[:pad] * gram_scale, values[pad:] * rhs_scale], axis=0)
-
-    def pass_on(turn):
-        send_x(turn).wait_recv()
-        z_code[turn] = encode(mine[turn] + decode(landed_x[turn]))
-        send_z(turn).start()
 
     def accumulated(*accs):
         narrow = [[accs[4 * mxu + 2 * side : 4 * mxu + 2 * side + 2] for side in range(2)] for mxu in range(2)]
@@ -354,28 +382,32 @@
             rhs = pltpu.matmul_pop(flat_acc[0][side]) + pltpu.matmul_pop(flat_acc[1][side])
             return jnp.concatenate([gram[:pad], rhs], axis=0)
 
-        def deliver(step, sums):
-            if not scatter:
-                start = pl.multiple_of(block_at(step) * WIDTH, WIDTH)
-                part_out[:, pl.ds(start, WIDTH)] = sums
-                return
-            turn = lax.div(step, 2)
-            theirs = for_partner(step)
-
-            @pl.when(theirs)
-            def _():
-                x_code[turn] = encode(sums)
-                send_x(turn).start()
-
-            @pl.when(jnp.logical_not(theirs))
-            def _():
-                mine[turn] = sums
+        def keep(step, sums):
+            start = pl.multiple_of(block_at(step) * WIDTH, WIDTH)
+            part_out[:, pl.ds(start, WIDTH)] = sums
+
+        def pass_across(step, sums):
+            x_code[step] = encode(sums)
+            send_x(step, level_of(step)).start()
+
+        def joined(step, sums):
+            level = level_of(step)
+            send_x(0, level).wait_recv()
+            return sums + decode(landed_x[level])
+
+        def pass_along(step, sums):
+            turn = step - levels
+            z_code[turn] = encode(joined(step, sums))
+            send_z(turn).start()
 
         for acc in accs:
             pltpu.matmul_pop(acc)
-        for place in range(4):
+        build(block_at(0), 0)
+        for copy in strips:
+            copy.wait()
+        pl.when(jnp.logical_not(early))(meet)
+        for place in range(3):
             load(place).wait()
-        build(block_at(0), 0)
         weigh(block_at(0), 0, 0)
         weigh(block_at(0), 0, 1)
         turn_over(0)
@@ -386,40 +418,46 @@
                 block = block_at(step)
                 following = block_at(jnp.minimum(step + 1, blocks - 1))
                 more = step + 1 < blocks
-                middle = stages // 2
                 build(following, 1 - side)
                 for stage in range(stages):
-                    if stage == middle:
+                    if stage == 1:
                         sums = result(1 - side)
+                        places = range(3 + 2 * side, 5 + 3 * side)
+
+                        @pl.when(turn == 0)
+                        def _():
+                            for place in places:
+                                load(place).wait()
+
                         if side == 1:
-
-                            @pl.when(turn == 0)
+                            pl.when(jnp.logical_and(early, turn == 0))(meet)
+
+                        if scatter:
+
+                            @pl.when(jnp.logical_and(step > 0, step <= levels))
                             def _():
-                                for place in range(4, blocks):
-                                    load(place).wait()
-
-                            deliver(step - 1, sums)
+                                pass_across(step - 1, sums)
+
+                            @pl.when(step > levels)
+                            def _():
+                                pass_along(step - 1, sums)
+
                         else:
 
-                            @pl.when(jnp.logical_and(early, turn == 1))
+                            @pl.when(step > 0)
                             def _():
-                                meet()
-
-                            @pl.when(turn > 0)
-                            def _():
-                                deliver(step - 1, sums)
-
-                            if scatter:
-
-                                @pl.when(turn > 1)
-                                def _():
-                                    pass_on(turn - 2)
-
-                        @pl.when(jnp.logical_and(more, following == 0))
+                                keep(step - 1, sums)
+
+                        @pl.when(jnp.logical_and(more, jnp.logical_and(following == 0, chan > 0)))
                         def _():
                             to_right.wait_recv()
 
-                        @pl.when(jnp.logical_and(more, following == blocks - 1))
+                        @pl.when(
+                            jnp.logical_and(
+                                more,
+                                jnp.logical_and(following == blocks - 1, chan < n_chan - 1),
+                            )
+                        )
                         def _():
                             to_left.wait_recv()
 
@@ -437,17 +475,13 @@
             for part in range(2):
                 for side in range(2):
                     pltpu.matmul_pop(narrow[mxu][side][part])
-        deliver(blocks - 1, result(1))
-
-    pl.run_scoped(accumulated, *acc_list(tall, flat))
-    to_left.wait_send()
-    to_right.wait_send()
-
-    if scatter:
-        pass_on(levels - 2)
-        last = levels - 1
-        send_x(last).wait_recv()
-        sums = mine[last] + decode(landed_x[last])
+        sums = result(1)
+        pl.when(chan > 0)(to_left.wait_send)
+        pl.when(chan < n_chan - 1)(to_right.wait_send)
+        if not scatter:
+            keep(blocks - 1, sums)
+            return
+        sums = joined(blocks - 1, sums)
         for turn in range(levels - 1):
             from_z(turn).wait_recv()
             sums = sums + decode(landed_z[level_at(turn)])
@@ -455,10 +489,12 @@
         for row, source in enumerate(mirror_rows(preds)):
             gram_out[row : row + 1, :] = total[source : source + 1, :]
         rhs_out[...] = total[pad : pad + preds, :]
-        for turn in range(levels):
-            send_x(turn).wait_send()
+        for step in range(levels):
+            send_x(step, 0).wait_send()
         for turn in range(levels - 1):
             send_z(turn).wait_send()
+
+    pl.run_scoped(accumulated, *acc_list(tall, flat))
 
 
 def acc_list(tall, flat):
@@ -501,6 +537,7 @@
         out_specs=tuple(vmem for _ in out_shape),
         scratch_shapes=[
             pltpu.VMEM((own + 4 * HALO, obs_dev), jnp.bfloat16),
+            pltpu.VMEM((2, HALO, obs_dev), jnp.bfloat16),
             pltpu.VMEM(predictors.shape, jnp.bfloat16),
             pltpu.VMEM(inv_band.shape, jnp.bfloat16),
             pltpu.VMEM((1, own + 2 * LANES), jnp.int32),
@@ -511,13 +548,12 @@
             pltpu.VMEM((2, LANES, TILE), jnp.float32),
             pltpu.VMEM((2, WIDTH, 2 * TILE), jnp.bfloat16),
             pltpu.VMEM((2, 2, OBS_TILE, WIDTH), jnp.bfloat16),
-            pltpu.VMEM(kept, jnp.float32),
             pltpu.VMEM(kept, jnp.int16),
             pltpu.VMEM(kept, jnp.int16),
             pltpu.VMEM(kept, jnp.int16),
             pltpu.VMEM(kept, jnp.int16),
             pltpu.VMEM((rows, WIDTH), jnp.float32),
-            dma((6,)),
+            dma((8,)),
             dma((blocks,)),
             dma((2,)),
             dma((2,)),

time: 21.5 us -> 19 us (0.88)
  the two profiles are of different devices: /device:TPU:20 before, /device:TPU:1 now
where the time goes in v2:
time: 19 us; the launch traced here: 18.8 us
  Pallas kernels  16.9 us (89%)
  local copies, waits for them, and re-layouts  1.25 us (7%)
  between operations  0.64 us (3%)
    pallas_call x1, Pallas kernels, on_device(): pl.pallas_call(functools.partial(kernel, n_obs, n_chan, scatter), out_sha...  16.9 us
    unnamed x2, local copies, waits for them, and re-layouts  1.25 us

profile of v2, /device:TPU:1, one launch (start us, length us, event | category | flops | bytes accessed | tf_op | source)
XLA Modules:
  0.0 18.8 jit_solution(14683124159114941407)
XLA Ops:
  0.6 16.9 %normal_equations.1 = (f32[100,256]{1,0:T(8,128)S(1)}, f32[10,256]{1,0:T(8,128)S(1)}) custom-call(bf16[2048,2048]{1,0:T(8,128)(2,1)} %dep.1, bf16[10,2048]{1,0:T(8,128)(2,1)} %pred_.1, bf16[63,2048]{1,0:T(8,128)(2,1)} %inv.1, s32[1,8192]{1,0:T(1,128)} %bitcast.1, s32[16]{0:T(128)} %counts.1), custom_call_target="tpu_custom_call" | custom-call | tf_op jit(solution)/shard_map/normal_equations/pallas_call | solution.py:533
  17.6 0.6 %copy.9 = f32[100,256]{1,0:T(8,128)} copy(f32[100,256]{1,0:T(8,128)S(1)} %get-tuple-element.2) | data formatting | bytes 204800
  18.2 0.6 %copy.10 = f32[10,256]{1,0:T(8,128)} copy(f32[10,256]{1,0:T(8,128)S(1)} %get-tuple-element.3) | data formatting | bytes 20480

commit v3 on v2

--- a/solution.py
+++ b/solution.py
@@ -56,12 +56,16 @@
         pairs_t,
         preds_t,
         flip,
+        spun,
         bands,
         turned_w,
+        mine,
         x_code,
         z_code,
+        d_code,
         landed_x,
         landed_z,
+        landed_d,
         total,
         small_sem,
         load_sem,
@@ -71,6 +75,8 @@
         x_recv,
         z_send,
         z_recv,
+        d_send,
+        d_recv,
     ) = rest
     own, obs_dev = dep.shape
     preds = pred.shape[0]
@@ -78,8 +84,8 @@
     half = offsets // 2
     upper = preds * (preds + 1) // 2
     pad = padded(upper, 8)
-    tall = pairs_t.shape[0]
-    flat = preds_t.shape[0]
+    tall = pairs_t.shape[1]
+    flat = preds_t.shape[1]
     blocks = own // WIDTH
     levels = blocks // 2
     stages = obs_dev // (2 * OBS_TILE)
@@ -99,39 +105,49 @@
         partner = me
     early = lev == 0 if scatter else me < 0
 
+    def is_any(step, choices):
+        found = step == choices[0]
+        for choice in choices[1:]:
+            found = jnp.logical_or(found, step == choice)
+        return found
+
+    def straight(step):
+        return jnp.logical_or(early, is_any(step, (0, 2)))
+
+    def across(step):
+        return jnp.logical_and(jnp.logical_not(early), is_any(step, (1, 3, 4)))
+
+    def level_across(step):
+        return jnp.where(step < 2, 1, step - 1)
+
     def level_at(turn):
-        turn = jnp.int32(turn)
-        return jnp.where(turn == levels - 1, lev, jnp.where(turn >= lev, turn + 1, turn))
-
-    def level_of(step):
-        step = jnp.int32(step)
-        if not scatter:
-            return lax.div(step, 2)
-        late_first = jnp.where(step < 2, 1 - step, step)
-        late_last = jnp.where(step == levels - 1, 0, step + 1)
-        late_mid = jnp.where(
-            step == levels - 1, levels - 1, jnp.where(step == levels - 2, 0, step + 1)
-        )
-        lead = jnp.where(
-            early,
-            jnp.where(col == 0, late_mid, late_last),
-            jnp.where(col == 0, step, late_first),
-        )
-        return jnp.where(step < levels, lead, level_at(step - levels))
+        shifted = jnp.where(turn + 1 >= lev, turn + 2, turn + 1)
+        return jnp.where(turn == levels - 2, lev, shifted)
+
+    def turn_along(step):
+        return step - 5
 
     def block_at(step):
         step = jnp.int32(step)
         if not scatter:
             return jnp.where(step < 2, 1 - step, step)
-        return 2 * level_of(step) + jnp.where(step < levels, 1 - col, col)
+        ahead = jnp.where(step == 4, 1, jnp.where(step < 4, step + 2, step + 1))
+        ahead = jnp.where(step == 5, 0, jnp.where(step > 5, step, ahead))
+        later = jnp.where(
+            is_any(step, (0, 2)),
+            jnp.where(step == 0, 1, 0),
+            jnp.where(
+                is_any(step, (1, 3, 4)),
+                2 * level_across(step) + 1 - col,
+                2 * level_at(turn_along(step)) + col,
+            ),
+        )
+        return jnp.where(early, ahead, later)
 
     def chunk_at(place):
         if not scatter:
             return place
-        turned_on = jnp.where(place < 3, place + 1, jnp.where(place == 3, 0, place))
-        return jnp.where(
-            early, lax.rem(2 - col + place, blocks), jnp.where(col == 0, place, turned_on)
-        )
+        return jnp.where(early, lax.rem(place + 1, blocks), place)
 
     barrier = pltpu.get_barrier_semaphore()
     for index in (left, right):
@@ -139,10 +155,23 @@
     greeted = 2
     if scatter:
         pl.semaphore_signal(barrier, inc=1, device_id=peer("obs", partner), device_id_type=MESH)
-        for turn in range(levels - 1):
-            index = 2 * level_at(turn) + col
+        for away in range(1, levels):
+            index = 2 * lax.rem(lev + away, levels) + col
             pl.semaphore_signal(barrier, inc=1, device_id=peer("obs", index), device_id_type=MESH)
-        greeted += levels
+
+        @pl.when(early)
+        def _():
+            for level in range(1, levels):
+                index = 2 * level + 1 - col
+                pl.semaphore_signal(
+                    barrier, inc=1, device_id=peer("obs", index), device_id_type=MESH
+                )
+
+        @pl.when(jnp.logical_not(early))
+        def _():
+            pl.semaphore_signal(barrier, inc=1, device_id=peer("obs", 1 - col), device_id_type=MESH)
+
+        greeted += levels + jnp.where(early, levels - 1, 1)
 
     base = pl.multiple_of(chan * own, own)
     smalls = [
@@ -165,7 +194,7 @@
             small_sem.at[5],
         ),
     ]
-    for copy in smalls:
+    for copy in smalls[:2]:
         copy.start()
 
     def load(place):
@@ -181,7 +210,7 @@
         pltpu.make_async_copy(dep.at[pl.ds(0, HALO), :], strip.at[0], small_sem.at[6]),
         pltpu.make_async_copy(dep.at[pl.ds(own - HALO, HALO), :], strip.at[1], small_sem.at[7]),
     ]
-    for copy in strips:
+    for copy in strips + smalls[2:]:
         copy.start()
     for place in range(3):
         load(place).start()
@@ -224,8 +253,6 @@
 
     smalls[0].wait()
     smalls[1].wait()
-    for place in range(3, blocks):
-        load(place).start()
     values = pred_in[...].astype(jnp.float32)
     first_row = 0
     for first in range(preds):
@@ -238,14 +265,16 @@
         at = pl.ds(pl.multiple_of(line * slots, slots), slots)
         slot = lax.broadcasted_iota(jnp.int32, (tall + flat, slots), 1)
         live = jnp.where(slot < counts_in[line], wide[:, at], 0.0).astype(jnp.bfloat16)
-        pairs_t[:, at] = live[:tall, :]
-        preds_t[:, at] = live[tall:, :]
+        pairs_t[line] = live[:tall, :]
+        preds_t[line] = live[tall:, :]
         return carry
 
     lax.fori_loop(0, lines, mask_line, 0, unroll=4)
 
-    for copy in smalls[2:]:
+    for copy in strips + smalls[2:]:
         copy.wait()
+    for place in range(3, 5):
+        load(place).start()
 
     @pl.when(chan == 0)
     def _():
@@ -255,13 +284,19 @@
     def _():
         ids_in[:, LANES + own :] = jnp.full((1, LANES), -1, jnp.int32)
 
-    def build(block, side):
+    def turn_band(block):
+        for part in range(2):
+            first = pl.multiple_of(block * WIDTH + part * TILE, TILE)
+            own_ids = ids_in[:, pl.ds(first + TILE, TILE)].astype(jnp.float32)
+            flip[part, 0:offsets, :] = inv_in[:, pl.ds(first, TILE)].astype(jnp.float32)
+            flip[part, 64:65, :] = own_ids
+            spun[part] = flip[part].T
+
+    def skew_band(block, side):
         for part in range(2):
             first = pl.multiple_of(block * WIDTH + part * TILE, TILE)
             near = ids_in[:, pl.ds(first, 3 * TILE)].astype(jnp.float32)
-            flip[part, 0:offsets, :] = inv_in[:, pl.ds(first, TILE)].astype(jnp.float32)
-            flip[part, 64:65, :] = near[:, TILE : 2 * TILE]
-            turned = flip[part].T
+            turned = spun[part]
             own_id = turned[:, 64:65]
             place = lax.broadcasted_iota(jnp.int32, turned.shape, 1)
             turned = jnp.where(place < offsets, turned, 0.0)
@@ -273,38 +308,63 @@
                 stride_axis=0,
             )
             same = near[:, TILE - HALO : 3 * TILE - HALO] == own_id
-            bands[side, part * TILE : (part + 1) * TILE, :] = jnp.where(same, skewed, 0.0).astype(
-                jnp.bfloat16
-            )
-
-    def send_x(step, level):
+            band = jnp.where(same, skewed, 0.0).astype(jnp.bfloat16)
+            bands[side, part, 0] = band[:, :LANES]
+            bands[side, part, 1] = band[:, LANES:]
+
+    def wide_of(ref, first, second):
+        return jnp.concatenate([ref[first, second, 0], ref[first, second, 1]], axis=1)
+
+    def paired(ref, at):
+        return jnp.concatenate([ref[at // LANES], ref[at // LANES + 1]], axis=1)
+
+    def send_x(level):
         return pltpu.make_async_remote_copy(
-            src_ref=x_code.at[step],
+            src_ref=x_code.at[level],
             dst_ref=landed_x.at[level],
-            send_sem=x_send.at[step],
+            send_sem=x_send.at[level],
             recv_sem=x_recv.at[level],
             device_id=peer("obs", partner),
             device_id_type=MESH,
         )
 
-    def send_z(turn):
+    def send_z(level):
         return pltpu.make_async_remote_copy(
-            src_ref=z_code.at[turn],
+            src_ref=z_code.at[level],
             dst_ref=landed_z.at[lev],
-            send_sem=z_send.at[turn],
+            send_sem=z_send.at[level],
             recv_sem=z_recv.at[lev],
-            device_id=peer("obs", 2 * level_at(turn) + col),
+            device_id=peer("obs", 2 * level + col),
             device_id_type=MESH,
         )
 
-    def from_z(turn):
-        sender = level_at(turn)
+    def from_z(level):
         return pltpu.make_async_remote_copy(
             src_ref=z_code.at[0],
-            dst_ref=landed_z.at[sender],
+            dst_ref=landed_z.at[level],
             send_sem=z_send.at[0],
-            recv_sem=z_recv.at[sender],
-            device_id=peer("obs", 2 * sender + col),
+            recv_sem=z_recv.at[level],
+            device_id=peer("obs", 2 * level + col),
+            device_id_type=MESH,
+        )
+
+    def send_straight(block):
+        return pltpu.make_async_remote_copy(
+            src_ref=d_code.at[block],
+            dst_ref=landed_d.at[me],
+            send_sem=d_send.at[block],
+            recv_sem=d_recv.at[me],
+            device_id=peer("obs", block),
+            device_id_type=MESH,
+        )
+
+    def from_straight(source):
+        return pltpu.make_async_remote_copy(
+            src_ref=d_code.at[0],
+            dst_ref=landed_d.at[source],
+            send_sem=d_send.at[0],
+            recv_sem=d_recv.at[source],
+            device_id=peer("obs", source),
             device_id_type=MESH,
         )
 
@@ -349,7 +409,7 @@
                     )
                     pltpu.matmul_acc_lhs(
                         narrow[mxu][stage % 2][part],
-                        bands[band, part * TILE : (part + 1) * TILE, :],
+                        wide_of(bands, band, part),
                         load_staged_rhs=part,
                     )
 
@@ -357,24 +417,22 @@
             for mxu in range(2):
                 for part in range(2):
                     weighted = pltpu.matmul_pop(narrow[mxu][stage % 2][part])
-                    turned_w[stage % 2, mxu, :, part * TILE : (part + 1) * TILE] = weighted.astype(
-                        jnp.bfloat16
-                    ).T
+                    turned_w[stage % 4, mxu, part] = weighted.astype(jnp.bfloat16).T
 
         def gather(side, stage):
             edge = jnp.bfloat16(huber_edge)
             for mxu in range(2):
                 at = (2 * stage + mxu) * OBS_TILE
-                weighted = turned_w[stage % 2, mxu]
+                weighted = wide_of(turned_w, stage % 4, mxu)
                 qc_weight = edge / jnp.maximum(jnp.abs(weighted), edge)
                 scaled = jnp.clip(weighted, -edge, edge)
                 pltpu.matmul_push_rhs(qc_weight, staging_register=0, mxu_index=mxu)
                 pltpu.matmul_acc_lhs(
-                    tall_acc[mxu][side], pairs_t[:, at : at + OBS_TILE], load_staged_rhs=0
+                    tall_acc[mxu][side], paired(pairs_t, at), load_staged_rhs=0
                 )
                 pltpu.matmul_push_rhs(scaled, staging_register=1, mxu_index=mxu)
                 pltpu.matmul_acc_lhs(
-                    flat_acc[mxu][side], preds_t[:, at : at + OBS_TILE], load_staged_rhs=1
+                    flat_acc[mxu][side], paired(preds_t, at), load_staged_rhs=1
                 )
 
         def result(side):
@@ -386,31 +444,59 @@
             start = pl.multiple_of(block_at(step) * WIDTH, WIDTH)
             part_out[:, pl.ds(start, WIDTH)] = sums
 
-        def pass_across(step, sums):
-            x_code[step] = encode(sums)
-            send_x(step, level_of(step)).start()
-
         def joined(step, sums):
-            level = level_of(step)
-            send_x(0, level).wait_recv()
+            level = level_at(turn_along(step))
+            send_x(level).wait_recv()
             return sums + decode(landed_x[level])
 
         def pass_along(step, sums):
-            turn = step - levels
-            z_code[turn] = encode(joined(step, sums))
-            send_z(turn).start()
+            level = level_at(turn_along(step))
+            z_code[level] = encode(joined(step, sums))
+            send_z(level).start()
+
+        def deliver(step, sums):
+            block = block_at(step)
+            own_block = jnp.logical_and(early, block == col)
+
+            @pl.when(jnp.logical_and(straight(step), own_block))
+            def _():
+                mine[...] = sums
+
+            @pl.when(jnp.logical_and(straight(step), jnp.logical_not(own_block)))
+            def _():
+                d_code[block] = encode(sums)
+                send_straight(block).start()
+
+            @pl.when(across(step))
+            def _():
+                level = level_across(step)
+                x_code[level] = encode(sums)
+                send_x(level).start()
+
+            @pl.when(jnp.logical_not(jnp.logical_or(straight(step), across(step))))
+            def _():
+                pass_along(step, sums)
 
         for acc in accs:
             pltpu.matmul_pop(acc)
-        build(block_at(0), 0)
-        for copy in strips:
-            copy.wait()
+        turn_band(block_at(0))
+        skew_band(block_at(0), 0)
         pl.when(jnp.logical_not(early))(meet)
+        for place in range(5, blocks):
+            load(place).start()
+        turned_w[2:] = jnp.zeros((2,) + turned_w.shape[1:], turned_w.dtype)
         for place in range(3):
             load(place).wait()
-        weigh(block_at(0), 0, 0)
-        weigh(block_at(0), 0, 1)
-        turn_over(0)
+        def half_step(block, side, half_at):
+            for stage in (2 * half_at, 2 * half_at + 1):
+                weigh(block, side, stage)
+            for stage in (2 * half_at, 2 * half_at + 1):
+                if half_at == 0:
+                    gather(1 - side, stages - 2 + stage)
+                else:
+                    gather(side, stage - 2)
+            for stage in (2 * half_at, 2 * half_at + 1):
+                turn_over(stage)
 
         def one_turn(turn, carry):
             for side in range(2):
@@ -418,81 +504,89 @@
                 block = block_at(step)
                 following = block_at(jnp.minimum(step + 1, blocks - 1))
                 more = step + 1 < blocks
-                build(following, 1 - side)
-                for stage in range(stages):
-                    if stage == 1:
-                        sums = result(1 - side)
-                        places = range(3 + 2 * side, 5 + 3 * side)
-
-                        @pl.when(turn == 0)
-                        def _():
-                            for place in places:
-                                load(place).wait()
-
-                        if side == 1:
-                            pl.when(jnp.logical_and(early, turn == 0))(meet)
-
-                        if scatter:
-
-                            @pl.when(jnp.logical_and(step > 0, step <= levels))
-                            def _():
-                                pass_across(step - 1, sums)
-
-                            @pl.when(step > levels)
-                            def _():
-                                pass_along(step - 1, sums)
-
-                        else:
-
-                            @pl.when(step > 0)
-                            def _():
-                                keep(step - 1, sums)
-
-                        @pl.when(jnp.logical_and(more, jnp.logical_and(following == 0, chan > 0)))
-                        def _():
-                            to_right.wait_recv()
-
-                        @pl.when(
-                            jnp.logical_and(
-                                more,
-                                jnp.logical_and(following == blocks - 1, chan < n_chan - 1),
-                            )
-                        )
-                        def _():
-                            to_left.wait_recv()
-
-                    ahead = stage + 2
-                    if ahead < stages:
-                        weigh(block, side, ahead)
+                turn_band(following)
+                half_step(block, side, 0)
+                sums = result(1 - side)
+                places = range(3 + 2 * side, 5 + 3 * side)
+
+                @pl.when(turn == 0)
+                def _():
+                    for place in places:
+                        load(place).wait()
+
+                if side == 1:
+                    pl.when(jnp.logical_and(early, turn == 0))(meet)
+
+                @pl.when(step > 0)
+                def _():
+                    if scatter:
+                        deliver(step - 1, sums)
                     else:
-                        weigh(following, 1 - side, ahead - stages)
-                    turn_over((stage + 1) % stages)
-                    gather(side, stage)
+                        keep(step - 1, sums)
+
+                @pl.when(jnp.logical_and(more, jnp.logical_and(following == 0, chan > 0)))
+                def _():
+                    to_right.wait_recv()
+
+                @pl.when(
+                    jnp.logical_and(
+                        more,
+                        jnp.logical_and(following == blocks - 1, chan < n_chan - 1),
+                    )
+                )
+                def _():
+                    to_left.wait_recv()
+
+                for half_at in range(1, stages // 2):
+                    half_step(block, side, half_at)
+                skew_band(following, 1 - side)
             return carry
 
         lax.fori_loop(0, levels, one_turn, 0)
-        for mxu in range(2):
-            for part in range(2):
-                for side in range(2):
-                    pltpu.matmul_pop(narrow[mxu][side][part])
+        for stage in range(stages - 2, stages):
+            gather(1, stage)
         sums = result(1)
         pl.when(chan > 0)(to_left.wait_send)
         pl.when(chan < n_chan - 1)(to_right.wait_send)
         if not scatter:
             keep(blocks - 1, sums)
             return
-        sums = joined(blocks - 1, sums)
-        for turn in range(levels - 1):
-            from_z(turn).wait_recv()
-            sums = sums + decode(landed_z[level_at(turn)])
-        total[...] = sums * (1.0 / float(obs_dev * n_obs))
-        for row, source in enumerate(mirror_rows(preds)):
-            gram_out[row : row + 1, :] = total[source : source + 1, :]
-        rhs_out[...] = total[pad : pad + preds, :]
-        for step in range(levels):
-            send_x(step, 0).wait_send()
-        for turn in range(levels - 1):
-            send_z(turn).wait_send()
+
+        def finish(sums):
+            total[...] = sums * (1.0 / float(obs_dev * n_obs))
+            for row, source in enumerate(mirror_rows(preds)):
+                gram_out[row : row + 1, :] = total[source : source + 1, :]
+            rhs_out[...] = total[pad : pad + preds, :]
+
+        @pl.when(early)
+        def _():
+            deliver(blocks - 1, sums)
+            whole = mine[...]
+            for away in range(1, n_obs):
+                source = lax.rem(me + away, n_obs)
+                from_straight(source).wait_recv()
+                whole = whole + decode(landed_d[source])
+            finish(whole)
+            for away in range(1, n_obs):
+                send_straight(lax.rem(me + away, n_obs)).wait_send()
+
+        @pl.when(jnp.logical_not(early))
+        def _():
+            whole = joined(blocks - 1, sums)
+            for source in range(2):
+                from_straight(source).wait_recv()
+                whole = whole + decode(landed_d[source])
+            for turn in range(levels - 2):
+                level = level_at(turn)
+                from_z(level).wait_recv()
+                whole = whole + decode(landed_z[level])
+            finish(whole)
+            for block in range(2):
+                send_straight(block).wait_send()
+            for turn in range(levels - 2):
+                send_z(level_at(turn)).wait_send()
+            for level in range(1, levels):
+                send_x(level).wait_send()
 
     pl.run_scoped(accumulated, *acc_list(tall, flat))
 
@@ -513,7 +607,7 @@
     n_chan = lax.axis_size("chan")
     share = own // n_obs
     blocks = own // WIDTH
-    scatter = share == WIDTH and n_obs % 2 == 0 and n_obs >= 8
+    scatter = share == WIDTH and n_obs == 8
     pad = padded(upper, 8)
     tall = padded(upper, 16)
     flat = padded(preds + 2, 16)
@@ -529,6 +623,7 @@
     hbm = pl.BlockSpec(memory_space=pltpu.HBM)
     levels = blocks // 2
     kept = (levels, rows, WIDTH) if scatter else (1, 8, LANES)
+    many = (n_obs,) + kept[1:] if scatter else kept
     dma = pltpu.SemaphoreType.DMA
     outs = pl.pallas_call(
         functools.partial(kernel, n_obs, n_chan, scatter),
@@ -543,15 +638,19 @@
             pltpu.VMEM((1, own + 2 * LANES), jnp.int32),
             pltpu.SMEM(line_counts.shape, jnp.int32),
             pltpu.VMEM((tall + flat, obs_dev), jnp.float32),
-            pltpu.VMEM((tall, obs_dev), jnp.bfloat16),
-            pltpu.VMEM((flat, obs_dev), jnp.bfloat16),
+            pltpu.VMEM((obs_dev // LANES, tall, LANES), jnp.bfloat16),
+            pltpu.VMEM((obs_dev // LANES, flat, LANES), jnp.bfloat16),
             pltpu.VMEM((2, LANES, TILE), jnp.float32),
-            pltpu.VMEM((2, WIDTH, 2 * TILE), jnp.bfloat16),
-            pltpu.VMEM((2, 2, OBS_TILE, WIDTH), jnp.bfloat16),
+            pltpu.VMEM((2, TILE, LANES), jnp.float32),
+            pltpu.VMEM((2, 2, 2, TILE, LANES), jnp.bfloat16),
+            pltpu.VMEM((4, 2, 2, OBS_TILE, LANES), jnp.bfloat16),
+            pltpu.VMEM((rows, WIDTH), jnp.float32),
             pltpu.VMEM(kept, jnp.int16),
             pltpu.VMEM(kept, jnp.int16),
+            pltpu.VMEM(many, jnp.int16),
             pltpu.VMEM(kept, jnp.int16),
             pltpu.VMEM(kept, jnp.int16),
+            pltpu.VMEM(many, jnp.int16),
             pltpu.VMEM((rows, WIDTH), jnp.float32),
             dma((8,)),
             dma((blocks,)),
@@ -561,6 +660,8 @@
             dma((levels,)),
             dma((levels,)),
             dma((levels,)),
+            dma((n_obs,)),
+            dma((n_obs,)),
         ],
         compiler_params=pltpu.CompilerParams(
             collective_id=0,

time: 19 us -> 18.1 us (0.953)
  the two profiles are of different devices: /device:TPU:1 before, /device:TPU:0 now
where the time goes in v3:
time: 18.1 us; the launch traced here: 18 us
  Pallas kernels  16.1 us (89%)
  local copies, waits for them, and re-layouts  1.25 us (7%)
  between operations  0.64 us (4%)
    pallas_call x1, Pallas kernels, on_device(): pl.pallas_call(functools.partial(kernel, n_obs, n_chan, scatter), out_sha...  16.1 us
    unnamed x2, local copies, waits for them, and re-layouts  1.25 us

profile of v3, /device:TPU:0, one launch (start us, length us, event | category | flops | bytes accessed | tf_op | source)
XLA Modules:
  0.0 18.0 jit_solution(8667822429004687253)
XLA Ops:
  0.6 16.1 %normal_equations.1 = (f32[100,256]{1,0:T(8,128)S(1)}, f32[10,256]{1,0:T(8,128)S(1)}) custom-call(bf16[2048,2048]{1,0:T(8,128)(2,1)} %dep.1, bf16[10,2048]{1,0:T(8,128)(2,1)} %pred_.1, bf16[63,2048]{1,0:T(8,128)(2,1)} %inv.1, s32[1,8192]{1,0:T(1,128)} %bitcast.1, s32[16]{0:T(128)} %counts.1), custom_call_target="tpu_custom_call" | custom-call | tf_op jit(solution)/shard_map/normal_equations/pallas_call | solution.py:628
  16.7 0.6 %copy.9 = f32[100,256]{1,0:T(8,128)} copy(f32[100,256]{1,0:T(8,128)S(1)} %get-tuple-element.2) | data formatting | bytes 204800
  17.4 0.6 %copy.10 = f32[10,256]{1,0:T(8,128)} copy(f32[10,256]{1,0:T(8,128)S(1)} %get-tuple-element.3) | data formatting | bytes 20480

commit v4 on v3

--- a/solution.py
+++ b/solution.py
@@ -39,12 +39,8 @@
 
 
 def kernel(n_obs, n_chan, scatter, dep, pred, inv, ids, counts, *rest):
-    if scatter:
-        gram_out, rhs_out = rest[:2]
-        rest = rest[2:]
-    else:
-        part_out = rest[0]
-        rest = rest[1:]
+    part_out = rest[0]
+    rest = rest[1:]
     (
         window,
         strip,
@@ -66,7 +62,6 @@
         landed_x,
         landed_z,
         landed_d,
-        total,
         small_sem,
         load_sem,
         halo_send,
@@ -197,13 +192,16 @@
     for copy in smalls[:2]:
         copy.start()
 
-    def load(place):
+    fore = obs_dev // stages * 2
+
+    def load(place, part):
         chunk = chunk_at(jnp.int32(place))
         start = pl.multiple_of(chunk * WIDTH, WIDTH)
+        at = pl.ds(0, fore) if part == 0 else pl.ds(fore, obs_dev - fore)
         return pltpu.make_async_copy(
-            dep.at[pl.ds(start, WIDTH), :],
-            window.at[pl.ds(start + HALO, WIDTH), :],
-            load_sem.at[place],
+            dep.at[pl.ds(start, WIDTH), at],
+            window.at[pl.ds(start + HALO, WIDTH), at],
+            load_sem.at[part, place],
         )
 
     strips = [
@@ -213,7 +211,7 @@
     for copy in strips + smalls[2:]:
         copy.start()
     for place in range(3):
-        load(place).start()
+        load(place, 0).start()
 
     to_left = pltpu.make_async_remote_copy(
         src_ref=strip.at[0],
@@ -253,6 +251,8 @@
 
     smalls[0].wait()
     smalls[1].wait()
+    for place in range(3):
+        load(place, 1).start()
     values = pred_in[...].astype(jnp.float32)
     first_row = 0
     for first in range(preds):
@@ -273,8 +273,9 @@
 
     for copy in strips + smalls[2:]:
         copy.wait()
-    for place in range(3, 5):
-        load(place).start()
+    for part in range(2):
+        for place in range(3, 5):
+            load(place, part).start()
 
     @pl.when(chan == 0)
     def _():
@@ -482,11 +483,12 @@
         turn_band(block_at(0))
         skew_band(block_at(0), 0)
         pl.when(jnp.logical_not(early))(meet)
-        for place in range(5, blocks):
-            load(place).start()
+        for part in range(2):
+            for place in range(5, blocks):
+                load(place, part).start()
         turned_w[2:] = jnp.zeros((2,) + turned_w.shape[1:], turned_w.dtype)
         for place in range(3):
-            load(place).wait()
+            load(place, 0).wait()
         def half_step(block, side, half_at):
             for stage in (2 * half_at, 2 * half_at + 1):
                 weigh(block, side, stage)
@@ -507,12 +509,15 @@
                 turn_band(following)
                 half_step(block, side, 0)
                 sums = result(1 - side)
-                places = range(3 + 2 * side, 5 + 3 * side)
+                due = [(place, 1) for place in range(3)] + [(3, 0), (4, 0)]
+                if side == 1:
+                    due = [(3, 1), (4, 1)]
+                    due += [(place, part) for part in range(2) for place in range(5, blocks)]
 
                 @pl.when(turn == 0)
                 def _():
-                    for place in places:
-                        load(place).wait()
+                    for place, part in due:
+                        load(place, part).wait()
 
                 if side == 1:
                     pl.when(jnp.logical_and(early, turn == 0))(meet)
@@ -553,10 +558,7 @@
             return
 
         def finish(sums):
-            total[...] = sums * (1.0 / float(obs_dev * n_obs))
-            for row, source in enumerate(mirror_rows(preds)):
-                gram_out[row : row + 1, :] = total[source : source + 1, :]
-            rhs_out[...] = total[pad : pad + preds, :]
+            part_out[...] = sums * (1.0 / float(obs_dev * n_obs))
 
         @pl.when(early)
         def _():
@@ -591,6 +593,18 @@
     pl.run_scoped(accumulated, *acc_list(tall, flat))
 
 
+def spread(preds, pad, part, gram_out, rhs_out, gram, rhs, sems):
+    rhs[...] = part[pad : pad + preds, :]
+    rhs_copy = pltpu.make_async_copy(rhs, rhs_out, sems.at[0])
+    rhs_copy.start()
+    for row, source in enumerate(mirror_rows(preds)):
+        gram[row : row + 1, :] = part[source : source + 1, :]
+    gram_copy = pltpu.make_async_copy(gram, gram_out, sems.at[1])
+    gram_copy.start()
+    rhs_copy.wait()
+    gram_copy.wait()
+
+
 def acc_list(tall, flat):
     specs = []
     for rows, copies in ((TILE, 4), (tall, 2), (flat, 2)):
@@ -613,10 +627,7 @@
     flat = padded(preds + 2, 16)
     rows = pad + flat
     if scatter:
-        out_shape = (
-            pltpu.VMEM((preds * preds, share), jnp.float32),
-            pltpu.VMEM((preds, share), jnp.float32),
-        )
+        out_shape = (pltpu.VMEM((rows, share), jnp.float32),)
     else:
         out_shape = (jax.ShapeDtypeStruct((rows, own), jnp.float32),)
     vmem = pl.BlockSpec(memory_space=pltpu.VMEM)
@@ -651,9 +662,8 @@
             pltpu.VMEM(kept, jnp.int16),
             pltpu.VMEM(kept, jnp.int16),
             pltpu.VMEM(many, jnp.int16),
-            pltpu.VMEM((rows, WIDTH), jnp.float32),
             dma((8,)),
-            dma((blocks,)),
+            dma((2, blocks)),
             dma((2,)),
             dma((2,)),
             dma((levels,)),
@@ -671,7 +681,22 @@
         name="normal_equations",
     )(departures, predictors, inv_band, band_id[None, :], line_counts)
     if scatter:
-        return outs[0], outs[1]
+        return pl.pallas_call(
+            functools.partial(spread, preds, pad),
+            out_shape=(
+                jax.ShapeDtypeStruct((preds * preds, share), jnp.float32),
+                jax.ShapeDtypeStruct((preds, share), jnp.float32),
+            ),
+            in_specs=[vmem],
+            out_specs=(hbm, hbm),
+            scratch_shapes=[
+                pltpu.VMEM((preds * preds, share), jnp.float32),
+                pltpu.VMEM((preds, share), jnp.float32),
+                dma((2,)),
+            ],
+            compiler_params=pltpu.CompilerParams(vmem_limit_bytes=1024 * 1024),
+            name="mirror",
+        )(outs[0])
     factor = 1.0 / float(obs_dev * n_obs)
     part = lax.psum_scatter(outs[0], "obs", scatter_dimension=1, tiled=True) * factor
     mirror = np.array(mirror_rows(preds))

time: 18.1 us -> 17.3 us (0.956)
  local copies, waits for them, and re-layouts: 1.25 us -> 0 us
  Pallas kernels: 16.1 us -> 16.5 us
    unnamed x2 -> x0, local copies, waits for them, and re-layouts: 1.25 us -> none
    pallas_call x0 -> x1, Pallas kernels: none -> 0.7 us  [on_device(): pl.pallas_call(functools.partial(spread, preds, pad), out_shape=(jax.Shap...]
    pallas_call x1, Pallas kernels: 16.1 us -> 15.8 us  [on_device(): pl.pallas_call(functools.partial(kernel, n_obs, n_chan, scatter), out_sha...]
where the time goes in v4:
time: 17.3 us; the launch traced here: 17.1 us
  Pallas kernels  16.5 us (95%)
  between operations  0.64 us (4%)
    pallas_call x1, Pallas kernels, on_device(): pl.pallas_call(functools.partial(kernel, n_obs, n_chan, scatter), out_sha...  15.8 us
    pallas_call x1, Pallas kernels, on_device(): pl.pallas_call(functools.partial(spread, preds, pad), out_shape=(jax.Shap...  0.7 us

profile of v4, /device:TPU:0, one launch (start us, length us, event | category | flops | bytes accessed | tf_op | source)
XLA Modules:
  0.0 17.1 jit_solution(9367165463977667622)
XLA Ops:
  0.6 15.8 %normal_equations.1.part = f32[72,256]{1,0:T(8,128)S(1)} custom-call(bf16[2048,2048]{1,0:T(8,128)(2,1)} %dep.1, bf16[10,2048]{1,0:T(8,128)(2,1)} %pred_.1, bf16[63,2048]{1,0:T(8,128)(2,1)} %inv.1, s32[1,8192]{1,0:T(1,128)} %bitcast.1, s32[16]{0:T(128)} %counts.1), custom_call_target="tpu_custom_call" | custom-call | tf_op jit(solution)/shard_map/normal_equations/pallas_call | solution.py:639
  16.4 0.7 %mirror.1 = (f32[100,256]{1,0:T(8,128)}, f32[10,256]{1,0:T(8,128)}) custom-call(f32[72,256]{1,0:T(8,128)S(1)} %normal_equations.1.part), custom_call_target="tpu_custom_call" | custom-call | tf_op jit(solution)/shard_map/mirror/pallas_call | solution.py:684

commit v5 on v4

--- a/solution.py
+++ b/solution.py
@@ -112,12 +112,12 @@
     def across(step):
         return jnp.logical_and(jnp.logical_not(early), is_any(step, (1, 3, 4)))
 
-    def level_across(step):
-        return jnp.where(step < 2, 1, step - 1)
-
     def level_at(turn):
         shifted = jnp.where(turn + 1 >= lev, turn + 2, turn + 1)
         return jnp.where(turn == levels - 2, lev, shifted)
+
+    def level_across(step):
+        return level_at(jnp.where(step < 2, 0, step - 2))
 
     def turn_along(step):
         return step - 5
@@ -126,8 +126,9 @@
         step = jnp.int32(step)
         if not scatter:
             return jnp.where(step < 2, 1 - step, step)
-        ahead = jnp.where(step == 4, 1, jnp.where(step < 4, step + 2, step + 1))
-        ahead = jnp.where(step == 5, 0, jnp.where(step > 5, step, ahead))
+        odd_end = jnp.where(step < 6, step - 4, jnp.where(step == 6, 7, 2))
+        even_end = jnp.where(step == 4, 2, jnp.where(step == 5, 7, 7 - step))
+        ahead = jnp.where(step < 4, 6 - step, jnp.where(col == 1, odd_end, even_end))
         later = jnp.where(
             is_any(step, (0, 2)),
             jnp.where(step == 0, 1, 0),
@@ -142,7 +143,9 @@
     def chunk_at(place):
         if not scatter:
             return place
-        return jnp.where(early, lax.rem(place + 1, blocks), place)
+        aside = jnp.where(place == 6, 3, jnp.where(is_any(place, (3, 4, 5)), place + 1, place))
+        later = jnp.where(jnp.logical_and(lev == 1, col == 0), aside, place)
+        return jnp.where(early, jnp.where(place < 3, blocks - 3 + place, blocks - 1 - place), later)
 
     barrier = pltpu.get_barrier_semaphore()
     for index in (left, right):
@@ -512,12 +515,13 @@
                 due = [(place, 1) for place in range(3)] + [(3, 0), (4, 0)]
                 if side == 1:
                     due = [(3, 1), (4, 1)]
-                    due += [(place, part) for part in range(2) for place in range(5, blocks)]
+                    due += [(place, part) for part in range(2) for place in range(6 - part, blocks)]
 
                 @pl.when(turn == 0)
                 def _():
                     for place, part in due:
                         load(place, part).wait()
+                    pl.when((lev == 1) == (side == 0))(load(5, 0).wait)
 
                 if side == 1:
                     pl.when(jnp.logical_and(early, turn == 0))(meet)

time: 17.3 us -> 17 us (0.983)
  Pallas kernels: 16.5 us -> 16.2 us
    pallas_call x1, Pallas kernels: 15.8 us -> 15.5 us  [on_device(): pl.pallas_call(functools.partial(kernel, n_obs, n_chan, scatter), out_sha...]
where the time goes in v5:
time: 17 us; the launch traced here: 16.8 us
  Pallas kernels  16.2 us (95%)
  between operations  0.64 us (4%)
    pallas_call x1, Pallas kernels, on_device(): pl.pallas_call(functools.partial(kernel, n_obs, n_chan, scatter), out_sha...  15.5 us
    pallas_call x1, Pallas kernels, on_device(): pl.pallas_call(functools.partial(spread, preds, pad), out_shape=(jax.Shap...  0.7 us

profile of v5, /device:TPU:0, one launch (start us, length us, event | category | flops | bytes accessed | tf_op | source)
XLA Modules:
  0.0 16.8 jit_solution(18417196740120111954)
XLA Ops:
  0.6 15.5 %normal_equations.1.part = f32[72,256]{1,0:T(8,128)S(1)} custom-call(bf16[2048,2048]{1,0:T(8,128)(2,1)} %dep.1, bf16[10,2048]{1,0:T(8,128)(2,1)} %pred_.1, bf16[63,2048]{1,0:T(8,128)(2,1)} %inv.1, s32[1,8192]{1,0:T(1,128)} %bitcast.1, s32[16]{0:T(128)} %counts.1), custom_call_target="tpu_custom_call" | custom-call | tf_op jit(solution)/shard_map/normal_equations/pallas_call | solution.py:643
  16.1 0.7 %mirror.1 = (f32[100,256]{1,0:T(8,128)}, f32[10,256]{1,0:T(8,128)}) custom-call(f32[72,256]{1,0:T(8,128)S(1)} %normal_equations.1.part), custom_call_target="tpu_custom_call" | custom-call | tf_op jit(solution)/shard_map/mirror/pallas_call | solution.py:688

commit v6 on v5

--- a/solution.py
+++ b/solution.py
@@ -515,13 +515,21 @@
                 due = [(place, 1) for place in range(3)] + [(3, 0), (4, 0)]
                 if side == 1:
                     due = [(3, 1), (4, 1)]
-                    due += [(place, part) for part in range(2) for place in range(6 - part, blocks)]
 
                 @pl.when(turn == 0)
                 def _():
                     for place, part in due:
                         load(place, part).wait()
-                    pl.when((lev == 1) == (side == 0))(load(5, 0).wait)
+                    pl.when(lev == 1)(load(5, side).wait)
+
+                if side == 0:
+
+                    @pl.when(turn == 1)
+                    def _():
+                        for part in range(2):
+                            pl.when(lev != 1)(load(5, part).wait)
+                            for place in range(6, blocks):
+                                load(place, part).wait()
 
                 if side == 1:
                     pl.when(jnp.logical_and(early, turn == 0))(meet)

time: 17 us -> 16.8 us (0.988)
  Pallas kernels: 16.2 us -> 16 us
where the time goes in v6:
time: 16.8 us; the launch traced here: 16.7 us
  Pallas kernels  16 us (95%)
  between operations  0.64 us (4%)
    pallas_call x1, Pallas kernels, on_device(): pl.pallas_call(functools.partial(kernel, n_obs, n_chan, scatter), out_sha...  15.3 us
    pallas_call x1, Pallas kernels, on_device(): pl.pallas_call(functools.partial(spread, preds, pad), out_shape=(jax.Shap...  0.7 us

profile of v6, /device:TPU:0, one launch (start us, length us, event | category | flops | bytes accessed | tf_op | source)
XLA Modules:
  0.0 16.7 jit_solution(17538529574973464040)
XLA Ops:
  0.6 15.3 %normal_equations.1.part = f32[72,256]{1,0:T(8,128)S(1)} custom-call(bf16[2048,2048]{1,0:T(8,128)(2,1)} %dep.1, bf16[10,2048]{1,0:T(8,128)(2,1)} %pred_.1, bf16[63,2048]{1,0:T(8,128)(2,1)} %inv.1, s32[1,8192]{1,0:T(1,128)} %bitcast.1, s32[16]{0:T(128)} %counts.1), custom_call_target="tpu_custom_call" | custom-call | tf_op jit(solution)/shard_map/normal_equations/pallas_call | solution.py:651
  16.0 0.7 %mirror.1 = (f32[100,256]{1,0:T(8,128)}, f32[10,256]{1,0:T(8,128)}) custom-call(f32[72,256]{1,0:T(8,128)S(1)} %normal_equations.1.part), custom_call_target="tpu_custom_call" | custom-call | tf_op jit(solution)/shard_map/mirror/pallas_call | solution.py:696
